TPU v7x, 32 devices: a whole 2x2x4 slice. The times are simulated.
32 devices in a mesh: gx: 8 (over z, y), gy: 4 (over x, core).
Axes of the slice: x: 2, y: 2, z: 4, core: 2. Of those that a mesh axis runs over, the one named last changes fastest.
Arguments:
- hidden: bfloat16 [4096, 14336], P('gx', 'gy'), may hold values from -6 to 6
- weight: bfloat16 [4096, 14336], P(None, 'gy'), may hold values from -0.0625 to 0.0625
- cotangent: bfloat16 [4096, 4096], P('gx', 'gy'), may hold values from -6 to 6
Outputs:
- output: bfloat16 [4096, 4096], P('gx', 'gy')
- hidden_grad: bfloat16 [4096, 14336], P('gx', 'gy')
- weight_grad: float32 [4096, 14336], P('gx', 'gy')
All inputs are finite; a program needn't handle non-finite values.
Results may differ from a plain program's by a relative error of at most 0.001.
Values may be sent and summed in bfloat16 or wider, within the bound.
A program may use at most 128 MiB of HBM per device.

v0:
```python
import jax
import jax.numpy as jnp
from jax import lax
from jax.sharding import PartitionSpec as P


def shards(hidden, weight, cotangent):
    tok_rows = hidden.shape[0]
    grad_scale = float(tok_rows * lax.axis_size("gx")) ** (-0.5)
    output_rows = lax.psum_scatter(
        lax.dot_general(
            weight, hidden, (((1,), (1,)), ((), ())), preferred_element_type=jnp.float32
        ),
        "gy",
        scatter_dimension=0,
        tiled=True,
    )
    output = output_rows.T.astype(jnp.bfloat16)
    cotangent_full = lax.all_gather(cotangent, "gy", axis=1, tiled=True)
    hidden_grad = jnp.dot(cotangent_full, weight, preferred_element_type=jnp.float32).astype(
        jnp.bfloat16
    )
    own_blocks = lax.all_to_all(cotangent_full, "gx", split_axis=1, concat_axis=0, tiled=True)
    summed = lax.dot_general(
        own_blocks,
        lax.all_gather(hidden, "gx", axis=0, tiled=True),
        (((0,), (0,)), ((), ())),
        preferred_element_type=jnp.float32,
    )
    weight_grad = summed * grad_scale
    return (output, hidden_grad, weight_grad)


def solution(mesh):
    return jax.shard_map(
        shards,
        mesh=mesh,
        in_specs=(P("gx", "gy"), P(None, "gy"), P("gx", "gy")),
        out_specs=(P("gx", "gy"), P("gx", "gy"), P("gx", "gy")),
        check_vma=False,
    )
```

profile of v0, /device:TPU:5, one launch (start us, length us, event | category | flops | bytes accessed | tf_op | source)
XLA Modules:
  0.0 715.4 jit_solution(5855176551937631784)
XLA Ops:
  7.2 0.0 all-gather.3.cloned.1.call-start
  7.2 2.3 copy.8
  9.5 0.0 all-gather.3.cloned.1.call-update
  9.5 0.0 reduce-scatter.2.cloned.1.call-start
  9.6 22.4 %fusion = f32[4096,512]{1,0:T(8,128)} fusion(bf16[4096,3584]{1,0:T(8,128)(2,1)} %param.4, bf16[512,3584]{1,0:T(8,128)(2,1)} %param.3), kind=kOutput, calls=%fused_computation.3 | convolution fusion | flops 15032385536 | bytes 41418752 | tf_op jit(solution)/shard_map/dot_general | solution.py:11
  32.0 0.0 reduce-scatter.2.cloned.1.call-update
  32.0 0.0 all-gather.5.cloned.1.call-start
  32.0 0.7 all-gather.5.cloned.1.call-update
  32.7 13.5 %all-gather.3.cloned.1.call-done = bf16[512,4096]{0,1:T(8,128)(2,1)} async-done(((bf16[512,1024]{0,1:T(8,128)(2,1)}), bf16[512,4096]{0,1:T(8,128)(2,1)}) %all-gather.3.cloned.1.call-update) | async-done | bytes 4194320 | tf_op jit(solution)/shard_map/all_gather | solution.py:19
  46.2 5.5 all-to-all-start
  51.7 25.7 %convolution_convert_fusion = bf16[512,3584]{1,0:T(8,128)(2,1)} fusion(bf16[512,4096]{0,1:T(8,128)(2,1)} %all-gather.3.cloned.1.call-done, bf16[4096,3584]{1,0:T(8,128)(2,1)} %param.4), kind=kOutput, calls=%fused_computation.1 | convolution fusion | flops 15034220544 | bytes 37224448 | tf_op jit(solution)/shard_map/dot_general | solution.py:20
  77.4 107.6 %all-to-all-done = bf16[512,8,512]{0,2,1:T(8,128)(2,1)} async-done(((bf16[512,8,512]{0,2,1:T(8,128)(2,1)}), bf16[512,8,512]{0,2,1:T(8,128)(2,1)}, u32[]{:S(2)}, u32[]{:S(2)}) %all-to-all-start) | async-done | bytes 4194336 | tf_op jit(solution)/shard_map/all_to_all | solution.py:23
  185.0 6.5 copy.9
  191.5 0.0 reduce-scatter.2.cloned.1.call-done
  191.5 1.7 convert_bitcast_fusion
  193.2 1.3 copy.10
  194.5 490.4 %all-gather.5.cloned.1.call-done = bf16[4096,3584]{1,0:T(8,128)(2,1)} async-done(((bf16[512,3584]{1,0:T(8,128)(2,1)}), bf16[4096,3584]{1,0:T(8,128)(2,1)}) %all-gather.5.cloned.1.call-update) | async-done | bytes 29360144 | tf_op jit(solution)/shard_map/all_gather | solution.py:26
  684.9 23.9 %convolution_multiply_fusion = f32[512,3584]{1,0:T(8,128)} fusion(bf16[4096,512]{1,0:T(8,128)(2,1)} %bitcast.12, bf16[4096,3584]{1,0:T(8,128)(2,1)} %all-gather.5.cloned.1.call-done), kind=kOutput, calls=%fused_computation | convolution fusion | flops 15034220544 | bytes 40894464 | tf_op jit(solution)/shard_map/dot_general | solution.py:24
Async XLA Ops:
  7.2 39.0 %all-gather.3.cloned.1.call-start = ((), (), s32[]{:S(2)}) async-start(), calls=%async_computation.3 | async-start | bytes 5242880 | tf_op jit(solution)/shard_map/all_gather | solution.py:19
  9.5 182.0 %reduce-scatter.2.cloned.1.call-start = ((), (), s32[]{:S(2)}) async-start(), calls=%async_computation.2 | async-start | bytes 10485760 | tf_op jit(solution)/shard_map/reduce_scatter | solution.py:10
  32.0 653.0 %all-gather.5.cloned.1.call-start = ((), (), s32[]{:S(2)}) async-start(), calls=%async_computation.4 | async-start | bytes 33030144 | tf_op jit(solution)/shard_map/all_gather | solution.py:26
  46.2 138.8 %all-to-all-start = ((bf16[512,8,512]{0,2,1:T(8,128)(2,1)}), bf16[512,8,512]{0,2,1:T(8,128)(2,1)}, u32[]{:S(2)}, u32[]{:S(2)}) async-start(bf16[512,8,512]{0,2,1:T(8,128)(2,1)} %bitcast.11), calls=%async_computation.1 | async-start | bytes 8388608 | tf_op jit(solution)/shard_map/all_to_all | solution.py:23
Sparse Core Ops, SparseCore 0:
  10.1 36.0 all-gather.2
  48.8 70.8 reduce-scatter.1
  121.2 563.7 all-gather.4
where the time goes:
time: 716 us; the launch traced here: 715 us
  waiting for transfers between devices  612 us (85%)
  matrix products  72 us (10%)
  between operations  13.7 us (2%)
  local copies, waits for them, and re-layouts  10.1 us (1%)
    all_gather x1, waiting for transfers between devices, shards(): lax.all_gather(hidden, 'gx', axis=0, tiled=True)  490 us
    all_to_all x1, waiting for transfers between devices, shards(): lax.all_to_all(cotangent_full, 'gx', split_axis=1, concat_axis=0, tiled=T...  108 us
    dot_general x1, matrix products, shards(): jnp.dot(cotangent_full, weight, preferred_element_type=jnp.float32)  25.7 us
    dot_general x1, matrix products, shards(): lax.dot_general(own_blocks, lax.all_gather(hidden, 'gx', axis=0, tiled=Tr...  23.9 us
    dot_general x1, matrix products, shards(): lax.dot_general(weight, hidden, (((1,), (1,)), ((), ())), preferred_eleme...  22.4 us
  transfers between devices with their start and end apart: 4, of which 3 were waited for; matrix products, arithmetic and copies ran while one was open for 8% of the time, Pallas kernels for 0%

commit v1 on v0

--- a/solution.py
+++ b/solution.py
@@ -20,7 +20,12 @@
     hidden_grad = jnp.dot(cotangent_full, weight, preferred_element_type=jnp.float32).astype(
         jnp.bfloat16
     )
-    own_blocks = lax.all_to_all(cotangent_full, "gx", split_axis=1, concat_axis=0, tiled=True)
+    own_blocks = jnp.concatenate(
+        lax.all_to_all(
+            jnp.stack(jnp.split(cotangent_full, lax.axis_size("gx"), axis=1)), "gx", 0, 0
+        ),
+        axis=0,
+    )
     summed = lax.dot_general(
         own_blocks,
         lax.all_gather(hidden, "gx", axis=0, tiled=True),

time: 716 us -> 721 us (level)
    reduce_scatter x1, waiting for transfers between devices: 0.01 us -> 28.9 us  [shards(): lax.psum_scatter(lax.dot_general(weight, hidden, (((1,), (1,)), ((), ()))...]
    all_to_all x1, waiting for transfers between devices: 108 us -> 83.8 us  [shards(): lax.all_to_all(jnp.stack(jnp.split(cotangent_full, lax.axis_size('gx'), a...]
    unnamed x2 -> x8, local copies, waits for them, and re-layouts: 3.59 us -> 14.7 us
    all_gather x1, waiting for transfers between devices: 490 us -> 483 us  [shards(): lax.all_gather(hidden, 'gx', axis=0, tiled=True)]
  transfers between devices with their start and end apart: 4 -> 4, of which waited for: 3 -> 4; matrix products, arithmetic and copies ran while one was open for 8% -> 9% of each run, Pallas kernels for 0% -> 0%
where the time goes in v1:
time: 721 us; the launch traced here: 719 us
  waiting for transfers between devices  611 us (85%)
  matrix products  70.2 us (10%)
  local copies, waits for them, and re-layouts  16.6 us (2%)
  between operations  13.8 us (2%)
    all_gather x1, waiting for transfers between devices, shards(): lax.all_gather(hidden, 'gx', axis=0, tiled=True)  483 us
    all_to_all x1, waiting for transfers between devices, shards(): lax.all_to_all(jnp.stack(jnp.split(cotangent_full, lax.axis_size('gx'), a...  83.8 us
    reduce_scatter x1, waiting for transfers between devices, shards(): lax.psum_scatter(lax.dot_general(weight, hidden, (((1,), (1,)), ((), ()))...  28.9 us
    dot_general x1, matrix products, shards(): lax.dot_general(own_blocks, lax.all_gather(hidden, 'gx', axis=0, tiled=Tr...  23.9 us
    dot_general x1, matrix products, shards(): jnp.dot(cotangent_full, weight, preferred_element_type=jnp.float32)  23.8 us
    dot_general x1, matrix products, shards(): lax.dot_general(weight, hidden, (((1,), (1,)), ((), ())), preferred_eleme...  22.5 us
    unnamed x8, local copies, waits for them, and re-layouts  14.7 us
  transfers between devices with their start and end apart: 4, of which 4 were waited for; matrix products, arithmetic and copies ran while one was open for 9% of the time, Pallas kernels for 0%

profile of v1, /device:TPU:5, one launch (start us, length us, event | category | flops | bytes accessed | tf_op | source)
XLA Modules:
  0.0 719.4 jit_solution(5019832398603892576)
XLA Ops:
  7.2 0.0 all-gather.3.cloned.1.call-start
  7.2 0.7 all-gather.3.cloned.1.call-update
  7.9 0.0 reduce-scatter.2.cloned.1.call-start
  7.9 22.5 %fusion.8 = f32[4096,512]{1,0:T(8,128)} fusion(bf16[4096,3584]{1,0:T(8,128)(2,1)} %param.4, bf16[512,3584]{1,0:T(8,128)(2,1)} %param.3), kind=kOutput, calls=%fused_computation.19 | convolution fusion | flops 15032385536 | bytes 41418752 | tf_op jit(solution)/shard_map/dot_general | solution.py:11
  30.5 0.0 reduce-scatter.2.cloned.1.call-update
  30.5 0.0 all-gather.5.cloned.1.call-start
  30.6 0.7 all-gather.5.cloned.1.call-update
  31.3 14.4 %all-gather.3.cloned.1.call-done = bf16[512,4096]{1,0:T(8,128)(2,1)} async-done(((bf16[512,1024]{1,0:T(8,128)(2,1)}), bf16[512,4096]{1,0:T(8,128)(2,1)}) %all-gather.3.cloned.1.call-update) | async-done | bytes 4194320 | tf_op jit(solution)/shard_map/all_gather | solution.py:19
  45.6 1.9 fusion.7
  47.5 1.9 fusion.6
  49.4 1.9 fusion.5
  51.2 1.9 fusion.4
  53.1 2.0 fusion.3
  55.1 1.9 fusion.2
  57.0 2.0 fusion.1
  59.0 2.0 fusion
  61.0 5.5 all-to-all-start
  66.5 23.8 %convolution_convert_fusion = bf16[512,3584]{1,0:T(8,128)(2,1)} fusion(bf16[512,4096]{1,0:T(8,128)(2,1)} %all-gather.3.cloned.1.call-done, bf16[4096,3584]{1,0:T(8,128)(2,1)} %param.4), kind=kOutput, calls=%fused_computation.1 | convolution fusion | flops 15034220544 | bytes 37224448 | tf_op jit(solution)/shard_map/dot_general | solution.py:20
  90.2 28.9 %reduce-scatter.2.cloned.1.call-done = f32[1024,512]{1,0:T(8,128)} async-done(((f32[4096,512]{1,0:T(8,128)}), f32[1024,512]{1,0:T(8,128)}) %reduce-scatter.2.cloned.1.call-update) | async-done | bytes 2097168 | tf_op jit(solution)/shard_map/reduce_scatter | solution.py:10
  119.1 1.7 convert_bitcast_fusion
  120.8 1.3 copy.6
  122.1 83.8 %all-to-all-done = bf16[8,512,512]{2,1,0:T(8,128)(2,1)} async-done(((bf16[8,512,512]{2,1,0:T(8,128)(2,1)}), bf16[8,512,512]{2,1,0:T(8,128)(2,1)}, u32[]{:S(2)}, u32[]{:S(2)}) %all-to-all-start) | async-done | bytes 4194336 | tf_op jit(solution)/shard_map/all_to_all | solution.py:24
  205.9 483.0 %all-gather.5.cloned.1.call-done = bf16[4096,3584]{1,0:T(8,128)(2,1)} async-done(((bf16[512,3584]{1,0:T(8,128)(2,1)}), bf16[4096,3584]{1,0:T(8,128)(2,1)}) %all-gather.5.cloned.1.call-update) | async-done | bytes 29360144 | tf_op jit(solution)/shard_map/all_gather | solution.py:31
  689.0 23.9 %convolution_multiply_fusion = f32[512,3584]{1,0:T(8,128)} fusion(bf16[4096,512]{1,0:T(8,128)(2,1)} %bitcast.9, bf16[4096,3584]{1,0:T(8,128)(2,1)} %all-gather.5.cloned.1.call-done), kind=kOutput, calls=%fused_computation | convolution fusion | flops 15034220544 | bytes 40894464 | tf_op jit(solution)/shard_map/dot_general | solution.py:29
Async XLA Ops:
  7.2 38.5 %all-gather.3.cloned.1.call-start = ((), (), s32[]{:S(2)}) async-start(), calls=%async_computation.3 | async-start | bytes 5242880 | tf_op jit(solution)/shard_map/all_gather | solution.py:19
  7.9 111.2 %reduce-scatter.2.cloned.1.call-start = ((), (), s32[]{:S(2)}) async-start(), calls=%async_computation.2 | async-start | bytes 10485760 | tf_op jit(solution)/shard_map/reduce_scatter | solution.py:10
  30.5 658.4 %all-gather.5.cloned.1.call-start = ((), (), s32[]{:S(2)}) async-start(), calls=%async_computation.4 | async-start | bytes 33030144 | tf_op jit(solution)/shard_map/all_gather | solution.py:31
  61.0 145.0 %all-to-all-start = ((bf16[8,512,512]{2,1,0:T(8,128)(2,1)}), bf16[8,512,512]{2,1,0:T(8,128)(2,1)}, u32[]{:S(2)}, u32[]{:S(2)}) async-start(bf16[8,512,512]{2,1,0:T(8,128)(2,1)} %fusion), calls=%async_computation.1 | async-start | bytes 8388608 | tf_op jit(solution)/shard_map/all_to_all | solution.py:24
Sparse Core Ops, SparseCore 0:
  9.5 36.0 all-gather.2
  48.2 70.8 reduce-scatter.1
  120.6 568.2 all-gather.4
